TPU v7x, 32 devices: a whole 2x2x4 slice. The times are simulated.
32 devices in a mesh: rep: 8 (over z, y), fsdp: 4 (over x, core).
Axes of the slice: x: 2, y: 2, z: 4, core: 2. Of those that a mesh axis runs over, the one named last changes fastest.
Arguments:
- gradients: bfloat16 [8, 4, 1024, 2048], P('rep', 'fsdp'), may hold values from -6 to 6
- momentum: float32 [8, 1024, 2048], P('rep', None, 'fsdp'), may hold values from -12 to 12
- master_weights: float32 [1024, 2048], P(None, 'fsdp'), may hold values from -0.125 to 0.125
Outputs:
- new_momentum: float32 [8, 1024, 2048], P('rep', None, 'fsdp')
- new_master: float32 [1024, 2048], P(None, 'fsdp')
- weights_full: bfloat16 [1024, 2048], replicated
All inputs are finite; a program needn't handle non-finite values.
Results may differ from a plain program's by a relative error of at most 0.012.
Values may be sent and summed in bfloat16 or wider, within the bound.
A program may use at most 128 MiB of HBM per device.

v0:
```python
import jax
import jax.numpy as jnp
from jax import lax
from jax.sharding import PartitionSpec as P

GROUP = 128
BAND = 16
momentum_decay = 0.9
step_size = 0.05


def cosine_rows():
    freq = jnp.arange(BAND, dtype=jnp.float32)[:, None]
    place = jnp.arange(GROUP, dtype=jnp.float32)[None, :]
    factor = jnp.where(freq == 0.0, jnp.sqrt(1.0 / GROUP), jnp.sqrt(2.0 / GROUP)).astype(
        jnp.float32
    )
    return factor * jnp.cos(jnp.pi * (2.0 * place + 1.0) * freq / (2.0 * GROUP))


def band_of(matrix):
    table = cosine_rows()
    blocks = matrix.reshape(matrix.shape[0] // GROUP, GROUP, matrix.shape[1] // GROUP, GROUP)
    return jnp.einsum("kr,arbc,lc->abkl", table, blocks, table, precision=lax.Precision.HIGHEST)


def spread_band(coeffs):
    table = cosine_rows()
    blocks = jnp.einsum("kr,abkl,lc->arbc", table, coeffs, table, precision=lax.Precision.HIGHEST)
    return blocks.reshape(coeffs.shape[0] * GROUP, coeffs.shape[1] * GROUP)


def local(gradients, momentum, master_weights):
    summed = lax.psum_scatter(
        gradients[0, 0].astype(jnp.float32).astype(jnp.bfloat16),
        "fsdp",
        scatter_dimension=1,
        tiled=True,
    ).astype(jnp.float32)
    moment = momentum_decay * momentum[0] + summed
    own_band = band_of(moment)
    remaining = moment - spread_band(own_band)
    mean_band = lax.psum(own_band, "rep") / lax.axis_size("rep")
    new_master = master_weights - step_size * spread_band(mean_band)
    weights_full = lax.all_gather(new_master.astype(jnp.bfloat16), "fsdp", axis=1, tiled=True)
    return (remaining[None], new_master, weights_full)


def solution(mesh):
    return jax.shard_map(
        local,
        mesh=mesh,
        in_specs=(P("rep", "fsdp", None, None), P("rep", None, "fsdp"), P(None, "fsdp")),
        out_specs=(P("rep", None, "fsdp"), P(None, "fsdp"), P()),
        check_vma=False,
    )
```

profile of v0, /device:TPU:0, one launch (start us, length us, event | category | flops | bytes accessed | tf_op | source)
XLA Modules:
  0.0 165.8 jit_solution(8107914245681863650)
XLA Ops:
  7.2 0.0 reduce-scatter.2.cloned.1.call-start
  7.2 6.4 %copy.7 = bf16[1,1,1024,2048]{2,3,1,0:T(8,128)(2,1)} copy(bf16[1,1,1024,2048]{3,2,1,0:T(8,128)(2,1)} %param.3) | data formatting | bytes 8388608 | tf_op args[0]
  13.6 0.0 reduce-scatter.2.cloned.1.call-update
  13.6 0.0 all-gather.2.cloned.1.call-start
  13.7 1.9 %copy.6 = f32[1,1024,512]{1,2,0:T(8,128)S(1)} copy(f32[1,1024,512]{2,1,0:T(8,128)} %param.4) | data formatting | bytes 4194304 | tf_op args[1]
  15.6 2.9 %copy.10 = f32[1024,512]{0,1:T(8,128)} copy(f32[1024,512]{1,0:T(8,128)} %param.5) | data formatting | bytes 4194304 | tf_op args[2]
  18.5 42.6 %reduce-scatter.2.cloned.1.call-done = bf16[1024,512]{0,1:T(8,128)(2,1)} async-done(((bf16[1024,2048]{0,1:T(8,128)(2,1)}), bf16[1024,512]{0,1:T(8,128)(2,1)}) %reduce-scatter.2.cloned.1.call-update) | async-done | bytes 1048592 | tf_op jit(solution)/shard_map/reduce_scatter | solution.py:34
  61.1 1.5 fusion.3
  62.6 0.5 copy.16
  63.1 1.8 %fusion.13 = f32[8,4,128,16]{3,0,2,1:T(8,128)S(1)} fusion(f32[8,128,4,128]{1,0,3,2:T(8,128)S(1)} %bitcast.56, f32[128]{0:T(128)S(1)} %add_multiply_fusion, f32[16]{0:T(128)S(1)} %compare_select_fusion), kind=kOutput, calls=%fused_computation.18 | convolution fusion | flops 100669440 | bytes 2359872 | tf_op jit(solution)/shard_map/kr,arbc,lc->abkl/dot_general | solution.py:24
  65.0 3.4 %fusion.1 = f32[8,4,16,16]{3,2,1,0:T(8,128)S(1)} fusion(f32[8,4,128,16]{3,0,2,1:T(8,128)S(1)} %fusion.13, f32[128]{0:T(128)S(1)} %add_multiply_fusion, f32[16]{0:T(128)S(1)} %compare_select_fusion), kind=kOutput, calls=%fused_computation.4 | convolution fusion | flops 12589056 | bytes 295488 | tf_op jit(solution)/shard_map/kr,arbc,lc->abkl/dot_general | solution.py:24
  68.4 40.2 %psum.7 = f32[8,4,16,16]{3,2,1,0:T(8,128)S(1)} all-reduce(f32[8,4,16,16]{3,2,1,0:T(8,128)S(1)} %fusion.1), channel_id=1, replica_groups=mesh['rep'=8,'fsdp'=4] {'rep'}, use_global_device_ids=true, to_apply=%region_1.2 | all-reduce | flops 8192 | bytes 65536 | tf_op jit(solution)/shard_map/psum | solution.py:43
  108.6 0.6 fusion.4
  109.2 4.8 %multiply_bitcast_fusion = f32[8,128,4,128]{3,1,2,0:T(8,128)} fusion(f32[8,4,16,128]{3,2,1,0:T(8,128)S(1)} %fusion.4, f32[128]{0:T(128)S(1)} %add_multiply_fusion, f32[16]{0:T(128)S(1)} %compare_select_fusion), kind=kOutput, calls=%fused_computation.6 | convolution fusion | flops 101193728 | bytes 2359872 | tf_op jit(solution)/shard_map/kr,abkl,lc->arbc/dot_general | solution.py:29
  114.0 2.9 %copy.9 = f32[8,128,4,128]{1,0,3,2:T(8,128)} copy(f32[8,128,4,128]{3,1,2,0:T(8,128)} %multiply_bitcast_fusion) | data formatting | bytes 4194304 | tf_op jit(solution)/shard_map/mul | solution.py:44
  116.9 4.7 %fusion.40 = (bf16[1024,512]{0,1:T(8,128)(2,1)}, f32[1024,512]{0,1:T(8,128)}) fusion(f32[1024,512]{0,1:T(8,128)} %copy.10, f32[64,8,8,128]{3,2,1,0:T(8,128)} %bitcast.54), kind=kLoop, calls=%fused_computation.48 | loop fusion | flops 1048576 | bytes 7340032 | tf_op jit(solution)/shard_map/convert_element_type | solution.py:45
  121.6 0.0 all-gather.2.cloned.1.call-update
  121.6 0.6 fusion.10
  122.2 4.8 %convolution_bitcast_fusion = f32[8,128,4,128]{3,1,2,0:T(8,128)} fusion(f32[8,4,16,128]{3,2,1,0:T(8,128)S(1)} %fusion.10, f32[128]{0:T(128)S(1)} %add_multiply_fusion, f32[16]{0:T(128)S(1)} %compare_select_fusion), kind=kOutput, calls=%fused_computation.7 | convolution fusion | flops 100669440 | bytes 2359872 | tf_op jit(solution)/shard_map/kr,abkl,lc->arbc/dot_general | solution.py:29
  127.0 0.0 copy-start.1
  127.0 3.1 %copy.8 = f32[8,128,4,128]{1,0,3,2:T(8,128)} copy(f32[8,128,4,128]{3,1,2,0:T(8,128)} %convolution_bitcast_fusion) | data formatting | bytes 4194304 | tf_op jit(solution)/shard_map/kr,abkl,lc->arbc/transpose | solution.py:29
  130.1 0.0 copy-done.1
  130.1 3.8 %fusion = f32[1,1024,512]{1,2,0:T(8,128)} fusion(f32[64,8,8,128]{3,2,1,0:T(8,128)} %bitcast.55, bf16[1024,512]{0,1:T(8,128)(2,1)S(1)} %copy-done.1, f32[1,1024,512]{1,2,0:T(8,128)S(1)} %copy.6), kind=kLoop, calls=%fused_computation.2 | loop fusion | flops 2097152 | bytes 7340032 | tf_op jit(solution)/shard_map/broadcast_in_dim | solution.py:46
  133.8 0.0 copy-start
  133.8 3.0 %copy.11 = f32[1,1024,512]{2,1,0:T(8,128)} copy(f32[1,1024,512]{1,2,0:T(8,128)} %fusion) | data formatting | bytes 4194304
  136.9 0.0 copy-done
  136.9 1.8 %copy.12 = f32[1024,512]{1,0:T(8,128)} copy(f32[1024,512]{0,1:T(8,128)S(1)} %copy-done) | data formatting | bytes 4194304
  138.7 13.9 %all-gather.2.cloned.1.call-done = bf16[1024,2048]{0,1:T(8,128)(2,1)} async-done(((bf16[1024,512]{0,1:T(8,128)(2,1)}), bf16[1024,2048]{0,1:T(8,128)(2,1)}) %all-gather.2.cloned.1.call-update) | async-done | bytes 4194320 | tf_op jit(solution)/shard_map/all_gather | solution.py:45
  152.6 6.4 %copy.13 = bf16[1024,2048]{1,0:T(8,128)(2,1)} copy(bf16[1024,2048]{0,1:T(8,128)(2,1)} %all-gather.2.cloned.1.call-done) | data formatting | bytes 8388608
  (2 shorter events, 0.0 us)
Async XLA Ops:
  7.2 53.9 %reduce-scatter.2.cloned.1.call-start = ((), (), s32[]{:S(2)}) async-start(), calls=%async_computation.1 | async-start | bytes 5242880 | tf_op jit(solution)/shard_map/reduce_scatter | solution.py:34
  13.6 139.0 %all-gather.2.cloned.1.call-start = ((), (), s32[]{:S(2)}) async-start(), calls=%async_computation.2 | async-start | bytes 5242880 | tf_op jit(solution)/shard_map/all_gather | solution.py:45
  127.0 3.1 %copy-start.1 = (bf16[1024,512]{0,1:T(8,128)(2,1)S(1)}, bf16[1024,512]{0,1:T(8,128)(2,1)}, u32[]{:S(2)}) copy-start(bf16[1024,512]{0,1:T(8,128)(2,1)} %reduce-scatter.2.cloned.1.call-done) | copy-start | bytes 3145732
  133.8 3.0 %copy-start = (f32[1024,512]{0,1:T(8,128)S(1)}, f32[1024,512]{0,1:T(8,128)}, u32[]{:S(2)}) copy-start(f32[1024,512]{0,1:T(8,128)} %get-tuple-element.7) | copy-start | bytes 6291460
Sparse Core Ops, SparseCore 0:
  13.8 47.2 reduce-scatter.1
  121.7 30.8 all-gather.1
where the time goes:
time: 166 us
  waiting for transfers between devices  56.5 us (34%)
  blocking collectives  40.2 us (24%)
  local copies, waits for them, and re-layouts  28.9 us (17%)
  matrix products  16 us (10%)
  between operations  14.1 us (8%)
  other arithmetic  10 us (6%)
    reduce_scatter x1, waiting for transfers between devices, local(): lax.psum_scatter(gradients[0, 0].astype(jnp.float32).astype(jnp.bfloat16)...  42.6 us
    psum x1, blocking collectives, local(): mean_band = lax.psum(own_band, 'rep') / lax.axis_size('rep')  40.2 us
    unnamed x11, local copies, waits for them, and re-layouts  22.9 us
    all_gather x1, waiting for transfers between devices, local(): lax.all_gather(new_master.astype(jnp.bfloat16), 'fsdp', axis=1, tiled=True)  13.9 us
    dot_general x4, matrix products, spread_band(): jnp.einsum('kr,abkl,lc->arbc', table, coeffs, table, precision=lax.Precis...  10.8 us
    dot_general x2, matrix products, band_of(): jnp.einsum('kr,arbc,lc->abkl', table, blocks, table, precision=lax.Precis...  5.25 us
    convert_element_type x1, other arithmetic, local(): new_master.astype(jnp.bfloat16)  4.72 us
    broadcast_in_dim x1, other arithmetic, local(): return (remaining[None], new_master, weights_full)  3.75 us
  transfers between devices with their start and end apart: 2, of which 2 were waited for; matrix products, arithmetic and copies ran while one was open for 13% of the time, Pallas kernels for 0%

commit v1 on v0

--- a/solution.py
+++ b/solution.py
@@ -40,7 +40,7 @@
     moment = momentum_decay * momentum[0] + summed
     own_band = band_of(moment)
     remaining = moment - spread_band(own_band)
-    mean_band = lax.psum(own_band, "rep") / lax.axis_size("rep")
+    mean_band = jnp.sum(lax.all_gather(own_band, "rep"), axis=0) / lax.axis_size("rep")
     new_master = master_weights - step_size * spread_band(mean_band)
     weights_full = lax.all_gather(new_master.astype(jnp.bfloat16), "fsdp", axis=1, tiled=True)
     return (remaining[None], new_master, weights_full)

time: 166 us -> 176 us (1.060)
  blocking collectives: 40.2 us -> 44.9 us
  waiting for transfers between devices: 56.5 us -> 59.2 us
  other arithmetic: 10 us -> 12 us
    all_gather x0 -> x1, blocking collectives: none -> 44.9 us  [local(): lax.all_gather(own_band, 'rep')]
    psum x1 -> x0, blocking collectives: 40.2 us -> none  [local(): mean_band = lax.psum(own_band, 'rep') / lax.axis_size('rep')]
    all_gather x1, waiting for transfers between devices: 13.9 us -> 16.6 us  [local(): lax.all_gather(new_master.astype(jnp.bfloat16), 'fsdp', axis=1, tiled=True)]
    reduce_sum x0 -> x1, other arithmetic: none -> 1.83 us  [local(): jnp.sum(lax.all_gather(own_band, 'rep'), axis=0) / lax.axis_size('rep')]
where the time goes in v1:
time: 176 us; the launch traced here: 175 us
  waiting for transfers between devices  59.2 us (34%)
  blocking collectives  44.9 us (26%)
  local copies, waits for them, and re-layouts  29 us (16%)
  matrix products  16 us (9%)
  between operations  14.1 us (8%)
  other arithmetic  12 us (7%)
    all_gather x1, blocking collectives, local(): lax.all_gather(own_band, 'rep')  44.9 us
    reduce_scatter x1, waiting for transfers between devices, local(): lax.psum_scatter(gradients[0, 0].astype(jnp.float32).astype(jnp.bfloat16)...  42.6 us
    unnamed x11, local copies, waits for them, and re-layouts  22.9 us
    all_gather x1, waiting for transfers between devices, local(): lax.all_gather(new_master.astype(jnp.bfloat16), 'fsdp', axis=1, tiled=True)  16.6 us
    dot_general x4, matrix products, spread_band(): jnp.einsum('kr,abkl,lc->arbc', table, coeffs, table, precision=lax.Precis...  10.8 us
    dot_general x2, matrix products, band_of(): jnp.einsum('kr,arbc,lc->abkl', table, blocks, table, precision=lax.Precis...  5.25 us
    convert_element_type x1, other arithmetic, local(): new_master.astype(jnp.bfloat16)  4.72 us
    broadcast_in_dim x1, other arithmetic, local(): return (remaining[None], new_master, weights_full)  3.84 us
  transfers between devices with their start and end apart: 2, of which 2 were waited for; matrix products, arithmetic and copies ran while one was open for 13% of the time, Pallas kernels for 0%

profile of v1, /device:TPU:0, one launch (start us, length us, event | category | flops | bytes accessed | tf_op | source)
XLA Modules:
  0.0 175.2 jit_solution(8242003757176742835)
XLA Ops:
  7.2 0.0 reduce-scatter.2.cloned.1.call-start
  7.2 6.4 %copy.25 = bf16[1,1,1024,2048]{2,3,1,0:T(8,128)(2,1)} copy(bf16[1,1,1024,2048]{3,2,1,0:T(8,128)(2,1)} %param.3) | data formatting | bytes 8388608 | tf_op args[0]
  13.6 0.0 reduce-scatter.2.cloned.1.call-update
  13.6 0.0 all-gather.3.cloned.1.call-start
  13.7 1.9 %copy.24 = f32[1,1024,512]{1,2,0:T(8,128)S(1)} copy(f32[1,1024,512]{2,1,0:T(8,128)} %param.4) | data formatting | bytes 4194304 | tf_op args[1]
  15.6 2.9 %copy.31 = f32[1024,512]{0,1:T(8,128)} copy(f32[1024,512]{1,0:T(8,128)} %param.5) | data formatting | bytes 4194304 | tf_op args[2]
  18.5 42.6 %reduce-scatter.2.cloned.1.call-done = bf16[1024,512]{0,1:T(8,128)(2,1)} async-done(((bf16[1024,2048]{0,1:T(8,128)(2,1)}), bf16[1024,512]{0,1:T(8,128)(2,1)}) %reduce-scatter.2.cloned.1.call-update) | async-done | bytes 1048592 | tf_op jit(solution)/shard_map/reduce_scatter | solution.py:34
  61.1 1.5 fusion.3
  62.6 0.5 copy.38
  63.1 1.8 %fusion.13 = f32[8,4,128,16]{3,0,2,1:T(8,128)S(1)} fusion(f32[8,128,4,128]{1,0,3,2:T(8,128)S(1)} %bitcast.58, f32[128]{0:T(128)S(1)} %add_multiply_fusion, f32[16]{0:T(128)S(1)} %compare_select_fusion), kind=kOutput, calls=%fused_computation.18 | convolution fusion | flops 100669440 | bytes 2359872 | tf_op jit(solution)/shard_map/kr,arbc,lc->abkl/dot_general | solution.py:24
  65.0 3.4 %fusion.1 = f32[8,4,16,16]{3,2,1,0:T(8,128)S(1)} fusion(f32[8,4,128,16]{3,0,2,1:T(8,128)S(1)} %fusion.13, f32[128]{0:T(128)S(1)} %add_multiply_fusion, f32[16]{0:T(128)S(1)} %compare_select_fusion), kind=kOutput, calls=%fused_computation.4 | convolution fusion | flops 12589056 | bytes 295488 | tf_op jit(solution)/shard_map/kr,arbc,lc->abkl/dot_general | solution.py:24
  68.4 44.9 %all-gather = f32[64,4,16,16]{3,2,1,0:T(8,128)} all-gather(f32[8,4,16,16]{3,2,1,0:T(8,128)S(1)} %fusion.1), channel_id=2, replica_groups=mesh['rep'=8,'fsdp'=4] {'rep'}, dimensions={0}, use_global_device_ids=true | all-gather | bytes 294912 | tf_op jit(solution)/shard_map/all_gather | solution.py:43
  113.3 1.8 %reduce_sum.9 = f32[8,4,16,16]{3,2,1,0:T(8,128)S(1)} reduce(f32[8,8,4,16,16]{4,3,2,1,0:T(8,128)} %bitcast.57, f32[]{:T(128)} %constant.10.clone.1), dimensions={0}, to_apply=%region_1.2 | reduce | flops 57344 | bytes 294916 | tf_op jit(solution)/shard_map/reduce_sum | solution.py:43
  115.1 0.6 fusion.4
  115.7 4.8 %multiply_bitcast_fusion = f32[8,128,4,128]{3,1,2,0:T(8,128)} fusion(f32[8,4,16,128]{3,2,1,0:T(8,128)S(1)} %fusion.4, f32[128]{0:T(128)S(1)} %add_multiply_fusion, f32[16]{0:T(128)S(1)} %compare_select_fusion), kind=kOutput, calls=%fused_computation.6 | convolution fusion | flops 101193728 | bytes 2359872 | tf_op jit(solution)/shard_map/kr,abkl,lc->arbc/dot_general | solution.py:29
  120.5 2.9 %copy.30 = f32[8,128,4,128]{1,0,3,2:T(8,128)} copy(f32[8,128,4,128]{3,1,2,0:T(8,128)} %multiply_bitcast_fusion) | data formatting | bytes 4194304 | tf_op jit(solution)/shard_map/mul | solution.py:44
  123.4 4.7 %fusion.40 = (bf16[1024,512]{0,1:T(8,128)(2,1)}, f32[1024,512]{0,1:T(8,128)}) fusion(f32[1024,512]{0,1:T(8,128)} %copy.31, f32[64,8,8,128]{3,2,1,0:T(8,128)} %bitcast.55), kind=kLoop, calls=%fused_computation.48 | loop fusion | flops 1048576 | bytes 7340032 | tf_op jit(solution)/shard_map/convert_element_type | solution.py:45
  128.1 0.0 all-gather.3.cloned.1.call-update
  128.1 0.6 fusion.10
  128.7 4.8 %convolution_bitcast_fusion = f32[8,128,4,128]{3,1,2,0:T(8,128)} fusion(f32[8,4,16,128]{3,2,1,0:T(8,128)S(1)} %fusion.10, f32[128]{0:T(128)S(1)} %add_multiply_fusion, f32[16]{0:T(128)S(1)} %compare_select_fusion), kind=kOutput, calls=%fused_computation.7 | convolution fusion | flops 100669440 | bytes 2359872 | tf_op jit(solution)/shard_map/kr,abkl,lc->arbc/dot_general | solution.py:29
  133.5 0.0 copy-start.1
  133.5 3.2 %copy.28 = f32[8,128,4,128]{1,0,3,2:T(8,128)} copy(f32[8,128,4,128]{3,1,2,0:T(8,128)} %convolution_bitcast_fusion) | data formatting | bytes 4194304 | tf_op jit(solution)/shard_map/kr,abkl,lc->arbc/transpose | solution.py:29
  136.7 0.0 copy-done.1
  136.7 3.8 %fusion = f32[1,1024,512]{1,2,0:T(8,128)} fusion(f32[64,8,8,128]{3,2,1,0:T(8,128)} %bitcast.56, bf16[1024,512]{0,1:T(8,128)(2,1)S(1)} %copy-done.1, f32[1,1024,512]{1,2,0:T(8,128)S(1)} %copy.24), kind=kLoop, calls=%fused_computation.2 | loop fusion | flops 2097152 | bytes 7340032 | tf_op jit(solution)/shard_map/broadcast_in_dim | solution.py:46
  140.5 0.0 copy-start
  140.5 3.0 %copy.32 = f32[1,1024,512]{2,1,0:T(8,128)} copy(f32[1,1024,512]{1,2,0:T(8,128)} %fusion) | data formatting | bytes 4194304
  143.6 0.0 copy-done
  143.6 1.8 %copy.33 = f32[1024,512]{1,0:T(8,128)} copy(f32[1024,512]{0,1:T(8,128)S(1)} %copy-done) | data formatting | bytes 4194304
  145.4 16.6 %all-gather.3.cloned.1.call-done = bf16[1024,2048]{0,1:T(8,128)(2,1)} async-done(((bf16[1024,512]{0,1:T(8,128)(2,1)}), bf16[1024,2048]{0,1:T(8,128)(2,1)}) %all-gather.3.cloned.1.call-update) | async-done | bytes 4194320 | tf_op jit(solution)/shard_map/all_gather | solution.py:45
  161.9 6.4 %copy.34 = bf16[1024,2048]{1,0:T(8,128)(2,1)} copy(bf16[1024,2048]{0,1:T(8,128)(2,1)} %all-gather.3.cloned.1.call-done) | data formatting | bytes 8388608
  (2 shorter events, 0.0 us)
Async XLA Ops:
  7.2 53.9 %reduce-scatter.2.cloned.1.call-start = ((), (), s32[]{:S(2)}) async-start(), calls=%async_computation.1 | async-start | bytes 5242880 | tf_op jit(solution)/shard_map/reduce_scatter | solution.py:34
  13.6 148.3 %all-gather.3.cloned.1.call-start = ((), (), s32[]{:S(2)}) async-start(), calls=%async_computation.2 | async-start | bytes 5242880 | tf_op jit(solution)/shard_map/all_gather | solution.py:45
  133.5 3.2 %copy-start.1 = (bf16[1024,512]{0,1:T(8,128)(2,1)S(1)}, bf16[1024,512]{0,1:T(8,128)(2,1)}, u32[]{:S(2)}) copy-start(bf16[1024,512]{0,1:T(8,128)(2,1)} %reduce-scatter.2.cloned.1.call-done) | copy-start | bytes 3145732
  140.5 3.0 %copy-start = (f32[1024,512]{0,1:T(8,128)S(1)}, f32[1024,512]{0,1:T(8,128)}, u32[]{:S(2)}) copy-start(f32[1024,512]{0,1:T(8,128)} %get-tuple-element.13) | copy-start | bytes 6291460
Sparse Core Ops, SparseCore 0:
  13.8 47.2 reduce-scatter.1
  128.2 33.6 all-gather.2
